TPU v7x, 32 devices: a whole 2x2x4 slice. The times are simulated.
32 devices in a mesh: owner: 16 (over z, x, core), rep: 2 (over y).
Axes of the slice: x: 2, y: 2, z: 4, core: 2. Of those that a mesh axis runs over, the one named last changes fastest.
Arguments:
- features: float32 [16384, 256], P(('owner', 'rep')), may hold values from -6 to 6
- group_ids: int32 [16384], P(('owner', 'rep')), may hold values from 0 to 65535, as said below
- survive: int32 [16384], P(('owner', 'rep')), may hold values from 0 to 1
- home_row: int32 [65536], replicated, may hold values from 0 to 65535, as said below
- hot_ids: int32 [256], replicated, may hold values from 0 to 65535, as said below
Outputs:
- group_out: float32 [65536, 256], P(('owner', 'rep'))
- group_count: float32 [65536], P(('owner', 'rep'))
- hot_out: float32 [256, 256], P('rep')
- hot_count: float32 [256], P('rep')
Inputs may be any that keep to these rules, and one draw needn't show every extreme that they name: home_row is a permutation of the groups. hot_ids holds 256 different groups. `group_ids`: among the rows of one device, 128 name hot groups, and at most 64 rows name non-hot groups g whose home_row[g] // 4096 is one and the same owner index; on every device some owners get exactly 64 such rows.
All inputs are finite; a program needn't handle non-finite values.
Results may differ from a plain program's by a relative error of at most 0.00007.
Values sent between devices are 32-bit elements; how exact they have to be, the bound alone decides.
A program may use at most 64 MiB of HBM per device.

v0:
```python
import jax
import jax.numpy as jnp
from jax import lax
from jax.sharding import PartitionSpec as P


def local(features, group_ids, survive, home_row, hot_ids):
    rows = features.shape[0]
    width = features.shape[1]
    owners = lax.axis_size("owner")
    own_groups = home_row.shape[0] // owners
    capacity = 2 * rows // owners
    live = survive == 1
    matches = group_ids[:, None] == hot_ids[None, :]
    is_hot = jnp.any(matches, axis=1)
    hot_table = jnp.where(matches & live[:, None], 1.0, 0.0).astype(jnp.float32)
    hot_part = lax.dot_general(
        hot_table,
        features,
        (((0,), (0,)), ((), ())),
        precision=lax.Precision.HIGHEST,
        preferred_element_type=jnp.float32,
    )
    hot_tally = jnp.sum(hot_table, axis=0)
    part_sum, part_tally = (
        lax.psum_scatter(hot_part, "rep", scatter_dimension=0, tiled=True),
        lax.psum_scatter(hot_tally, "rep", scatter_dimension=0, tiled=True),
    )
    hot_sum, hot_count = lax.psum((part_sum, part_tally), "owner")
    hot_out = hot_sum / jnp.sqrt(1.0 + hot_count)[:, None]
    keep = live & jnp.logical_not(is_hot)
    destination = home_row[group_ids]
    target = destination // own_groups
    local_row = (destination % own_groups).astype(jnp.float32)
    member = (
        (target[:, None] == jnp.arange(owners, dtype=jnp.int32)[None, :]) & keep[:, None]
    ).astype(jnp.int32)
    position = jnp.cumsum(member, axis=0) - 1
    placed = jnp.sum(position * member, axis=1)
    target_safe = jnp.where(keep, target, owners)
    placed_safe = jnp.where(keep, placed, 0)
    bucket = (
        jnp.zeros((owners, capacity, width), jnp.float32)
        .at[target_safe, placed_safe]
        .set(features, mode="drop")
    )
    labels = (
        jnp.full((owners, capacity), -1.0, jnp.float32)
        .at[target_safe, placed_safe]
        .set(local_row, mode="drop")
    )
    arrived, arrived_labels = (
        lax.all_to_all(bucket, "owner", split_axis=0, concat_axis=0, tiled=True),
        lax.all_to_all(labels, "owner", split_axis=0, concat_axis=0, tiled=True),
    )
    total_rows = owners * capacity
    block = min(512, total_rows)
    flat_rows = arrived.reshape(total_rows // block, block, width)
    flat_labels = arrived_labels.astype(jnp.int32).reshape(total_rows // block, block)
    columns = jnp.arange(own_groups, dtype=jnp.int32)

    def add_block(carry, item):
        total, tally = carry
        block_rows, block_labels = item
        onehot = (block_labels[:, None] == columns[None, :]).astype(jnp.float32)
        total = total + lax.dot_general(
            onehot,
            block_rows,
            (((0,), (0,)), ((), ())),
            precision=lax.Precision.HIGHEST,
            preferred_element_type=jnp.float32,
        )
        tally = tally + jnp.sum(onehot, axis=0)
        return ((total, tally), None)

    start_carry = (
        jnp.zeros((own_groups, width), jnp.float32),
        jnp.zeros((own_groups,), jnp.float32),
    )
    (dense, dense_tally), _ = lax.scan(add_block, start_carry, (flat_rows, flat_labels))
    cold_sum, group_count = (
        lax.psum_scatter(dense, "rep", scatter_dimension=0, tiled=True),
        lax.psum_scatter(dense_tally, "rep", scatter_dimension=0, tiled=True),
    )
    group_out = cold_sum / jnp.sqrt(1.0 + group_count)[:, None]
    return (group_out, group_count, hot_out, hot_count)


def solution(mesh):
    in_specs = (P(("owner", "rep"), None), P(("owner", "rep")), P(("owner", "rep")), P(), P())
    out_specs = (P(("owner", "rep"), None), P(("owner", "rep")), P("rep", None), P("rep"))
    return jax.shard_map(local, mesh=mesh, in_specs=in_specs, out_specs=out_specs, check_vma=False)
```

profile of v0, /device:TPU:0, one launch (start us, length us, event | category | flops | bytes accessed | tf_op | source)
XLA Modules:
  0.0 341.8 jit_solution(15533062784439949146)
XLA Ops:
  7.2 0.8 compare_select_fusion.2
  8.0 0.9 compare_reduce_fusion
  8.9 3.1 gather_fusion
  12.1 0.7 compare_select_fusion.1
  12.8 1.2 reduce-window.6
  14.9 72.8 %scatter_fusion = f32[16,64]{1,0:T(8,128)} fusion(f32[16,64]{1,0:T(8,128)} %broadcast_in_dim.48, s32[512]{0:T(512)S(1)} %bitcast.49, f32[512]{0:T(512)S(1)} %get-tuple-element.77), kind=kCustom, calls=%fused_computation.1 | custom fusion | bytes 10240 | tf_op jit(solution)/shard_map/scatter | solution.py:50
  87.7 9.5 %all-to-all-start = ((f32[16,1,64]{2,1,0:T(1,128)}), f32[16,1,64]{2,1,0:T(1,128)S(1)}, u32[]{:S(2)}, u32[]{:S(2)}) async-start(f32[16,1,64]{2,1,0:T(1,128)} %bitcast.7), calls=%async_computation | async-start | bytes 16384 | tf_op jit(solution)/shard_map/all_to_all | solution.py:54
  97.2 1.1 broadcast_in_dim.53
  98.3 62.2 %scatter_fusion.1 = f32[16,64,256]{2,1,0:T(8,128)} fusion(f32[16,64,256]{2,1,0:T(8,128)} %broadcast_in_dim.53, s32[512]{0:T(512)S(1)} %bitcast.50, f32[512,256]{1,0:T(8,128)S(1)} %copy-done.1), kind=kCustom, calls=%fused_computation.2 | custom fusion | bytes 1576960 | tf_op jit(solution)/shard_map/scatter | solution.py:45
  160.5 6.0 %all-to-all-start.1 = ((f32[16,64,256]{2,1,0:T(8,128)}), f32[16,64,256]{2,1,0:T(8,128)S(1)}, u32[]{:S(2)}, u32[]{:S(2)}) async-start(f32[16,64,256]{2,1,0:T(8,128)} %scatter_fusion.1), calls=%async_computation.1 | async-start | bytes 2097152 | tf_op jit(solution)/shard_map/all_to_all | solution.py:53
  166.5 1.6 fusion.10
  168.4 13.6 %reduce-scatter.5.cloned.1.call-done = f32[128,256]{1,0:T(8,128)} async-done(((f32[256,256]{1,0:T(8,128)}), f32[128,256]{1,0:T(8,128)}) %reduce-scatter.5.cloned.1.call-update) | async-done | bytes 131088 | tf_op jit(solution)/shard_map/reduce_scatter | solution.py:26
  182.0 7.3 %all-to-all-done.1 = f32[16,64,256]{2,1,0:T(8,128)S(1)} async-done(((f32[16,64,256]{2,1,0:T(8,128)}), f32[16,64,256]{2,1,0:T(8,128)S(1)}, u32[]{:S(2)}, u32[]{:S(2)}) %all-to-all-start.1) | async-done | bytes 1048608 | tf_op jit(solution)/shard_map/all_to_all | solution.py:53
  189.3 22.5 %while.13 = (s32[]{:T(128)}, f32[4096,256]{1,0:T(8,128)}, f32[4096]{0:T(1024)S(1)}, s32[2,512]{1,0:T(2,128)S(1)}, f32[2,512,256]{2,1,0:T(8,128)S(1)}, /*index=5*/s32[]{:T(128)}, s32[]{:T(128)}) while((s32[]{:T(128)}, f32[4096,256]{1,0:T(8,128)}, f32[4096]{0:T(1024)S(1)}, s32[2,512]{1,0:T(2,128)S(1)}, f32[2,512,256]{2,1,0:T(8,128)S(1)}, ...), condition=%wide.region_8.9_spmd.clone, body=%wide.region_6.8_spmd.clone.sunk | while | flops 6452940800 | bytes 8986720 | solution.py:80
  189.3 8.5 %fusion.35 = f32[4096,256]{1,0:T(8,128)} fusion(f32[4096,256]{1,0:T(8,128)} %get-tuple-element.117, s32[512]{0:T(512)S(1)} %bitcast.52, pred[]{:T(512)S(6)} %compare.22, f32[2,512,256]{2,1,0:T(8,128)S(1)} %get-tuple-element.127, s32[]{:T(128)} %get-tuple-element.116), kind=kOutput, calls=%fused_computation.8.clone.1 | convolution fusion | flops 6446645248 | bytes 8914949 | tf_op jit(solution)/shard_map/while/body/eval_jaxpr/dot_general | solution.py:66
  197.8 2.0 fusion.36
  199.8 10.0 %fusion.35 = f32[4096,256]{1,0:T(8,128)} fusion(f32[4096,256]{1,0:T(8,128)} %get-tuple-element.117, s32[512]{0:T(512)S(1)} %bitcast.52, pred[]{:T(512)S(6)} %compare.22, f32[2,512,256]{2,1,0:T(8,128)S(1)} %get-tuple-element.127, s32[]{:T(128)} %get-tuple-element.116), kind=kOutput, calls=%fused_computation.8.clone.1 | convolution fusion | flops 6446645248 | bytes 8914949 | tf_op jit(solution)/shard_map/while/body/eval_jaxpr/dot_general | solution.py:66
  209.9 2.0 fusion.36
  214.6 7.6 %all-reduce.2 = (f32[4096]{0:T(1024)S(1)}, f32[256]{0:T(256)S(1)}) all-reduce(f32[4096]{0:T(1024)S(1)} %get-tuple-element.38, f32[256]{0:T(256)S(1)} %select_reduce_fusion), channel_id=3, replica_groups=mesh['owner'=16,'rep'=2] {'rep'}, use_global_device_ids=true, to_apply=%region_10.11.clone | all-reduce | flops 4352 | bytes 34816
  222.3 33.1 %psum.15 = f32[128]{0:T(128)S(1)} all-reduce(f32[128]{0:T(128)S(1)} %dynamic-slice.3), channel_id=1, replica_groups=mesh['owner'=16,'rep'=2] {'owner'}, use_global_device_ids=true, to_apply=%region_15.16 | all-reduce | flops 128 | bytes 1024 | tf_op jit(solution)/shard_map/psum | solution.py:29
  256.1 17.7 %all-reduce.5.cloned.1.call-done = f32[128,256]{1,0:T(8,128)} async-done(((f32[128,256]{1,0:T(8,128)}), f32[128,256]{1,0:T(8,128)}) %all-reduce.5.cloned.1.call-update) | async-done | bytes 131088 | tf_op jit(solution)/shard_map/psum | solution.py:29
  273.7 1.6 broadcast_divide_fusion.1
  275.4 56.6 %reduce-scatter.3.cloned.1.call-done = f32[2048,256]{1,0:T(8,128)} async-done(((f32[4096,256]{1,0:T(8,128)}), f32[2048,256]{1,0:T(8,128)}) %reduce-scatter.3.cloned.1.call-update) | async-done | bytes 2097168 | tf_op jit(solution)/shard_map/reduce_scatter | solution.py:82
  332.0 3.3 broadcast_divide_fusion
  (42 shorter events, 3.4 us)
Async XLA Ops:
  7.2 1.7 copy-start
  7.2 91.1 %copy-start.1 = (f32[512,256]{1,0:T(8,128)S(1)}, f32[512,256]{1,0:T(8,128)}, u32[]{:S(2)}) copy-start(f32[512,256]{1,0:T(8,128)} %param.7) | copy-start | bytes 1572868
  87.7 72.7 %all-to-all-start = ((f32[16,1,64]{2,1,0:T(1,128)}), f32[16,1,64]{2,1,0:T(1,128)S(1)}, u32[]{:S(2)}, u32[]{:S(2)}) async-start(f32[16,1,64]{2,1,0:T(1,128)} %bitcast.7), calls=%async_computation | async-start | bytes 16384 | tf_op jit(solution)/shard_map/all_to_all | solution.py:54
  98.3 68.2 %copy-start.2 = (s32[512]{0:T(512)S(1)}, s32[512]{0:T(512)}, u32[]{:S(2)}) copy-start(s32[512]{0:T(512)} %param.8) | copy-start | bytes 6148
  98.3 68.2 %copy-start.3 = (s32[256]{0:T(256)S(1)}, s32[256]{0:T(256)}, u32[]{:S(2)}) copy-start(s32[256]{0:T(256)} %param.11) | copy-start | bytes 3076
  160.5 28.9 %all-to-all-start.1 = ((f32[16,64,256]{2,1,0:T(8,128)}), f32[16,64,256]{2,1,0:T(8,128)S(1)}, u32[]{:S(2)}, u32[]{:S(2)}) async-start(f32[16,64,256]{2,1,0:T(8,128)} %scatter_fusion.1), calls=%async_computation.1 | async-start | bytes 2097152 | tf_op jit(solution)/shard_map/all_to_all | solution.py:53
  166.5 15.5 %reduce-scatter.5.cloned.1.call-start = ((), (), s32[]{:S(2)}) async-start(), calls=%async_computation.5 | async-start | bytes 393216 | tf_op jit(solution)/shard_map/reduce_scatter | solution.py:26
  168.2 105.5 %all-reduce.5.cloned.1.call-start = ((), (), s32[]{:S(2)}) async-start(), calls=%async_computation.6 | async-start | bytes 262144 | tf_op jit(solution)/shard_map/psum | solution.py:29
  182.0 150.0 %reduce-scatter.3.cloned.1.call-start = ((), (), s32[]{:S(2)}) async-start(), calls=%async_computation.4 | async-start | bytes 6291456 | tf_op jit(solution)/shard_map/reduce_scatter | solution.py:82
  211.9 0.7 copy-start.4
  255.5 79.8 %copy-start.5 = (f32[128]{0:T(128)}, f32[128]{0:T(128)S(1)}, u32[]{:S(2)}) copy-start(f32[128]{0:T(128)S(1)} %psum.15) | copy-start | bytes 1540
Sparse Core Ops, SparseCore 0:
  169.5 12.4 reduce-scatter.4
  185.4 88.2 all-reduce.4
  276.0 55.9 reduce-scatter.2
where the time goes:
time: 346 us; the launch traced here: 342 us
  local copies, waits for them, and re-layouts  141 us (41%)
  waiting for transfers between devices  95.2 us (28%)
  blocking collectives  40.7 us (12%)
  matrix products  20.1 us (6%)
  starting transfers between devices  15.6 us (5%)
  between operations  15.2 us (4%)
  other arithmetic  13.5 us (4%)
    scatter x1, local copies, waits for them, and re-layouts, local(): labels = jnp.full((owners, capacity), -1.0, jnp.float32).at[target_safe,...  72.8 us
    scatter x1, local copies, waits for them, and re-layouts, local(): bucket = jnp.zeros((owners, capacity, width), jnp.float32).at[target_safe...  62.2 us
    reduce_scatter x1, waiting for transfers between devices, local(): lax.psum_scatter(dense, 'rep', scatter_dimension=0, tiled=True)  56.6 us
    psum x1, blocking collectives, local(): hot_sum, hot_count = lax.psum((part_sum, part_tally), 'owner')  33.1 us
    dot_general x2, matrix products, add_block(): lax.dot_general(onehot, block_rows, (((0,), (0,)), ((), ())), precision=l...  18.5 us
    psum x1, waiting for transfers between devices, local(): hot_sum, hot_count = lax.psum((part_sum, part_tally), 'owner')  17.7 us
    reduce_scatter x1, waiting for transfers between devices, local(): lax.psum_scatter(hot_part, 'rep', scatter_dimension=0, tiled=True)  13.6 us
    all_to_all x1, starting transfers between devices, local(): lax.all_to_all(labels, 'owner', split_axis=0, concat_axis=0, tiled=True)  9.47 us
  transfers between devices with their start and end apart: 5, of which 4 were waited for; matrix products, arithmetic and copies ran while one was open for 27% of the time, Pallas kernels for 0%

commit v1 on v0

v1 whole, which is shorter than its diff:
```python
import functools

import jax
import jax.numpy as jnp
from jax import lax
from jax.experimental import pallas as pl
from jax.experimental.pallas import tpu as pltpu
from jax.sharding import PartitionSpec as P

MESH = pl.DeviceIdType.MESH
LANES = 128
SUB = 8
BF = jnp.bfloat16
F32 = jnp.float32


def iota(shape, axis):
    return lax.broadcasted_iota(jnp.int32, shape, axis)


def mm(a, b, dims=((1,), (0,))):
    return lax.dot_general(a, b, (dims, ((), ())), preferred_element_type=F32)


def split(x):
    hi = x.astype(BF)
    return hi, (x - hi.astype(F32)).astype(BF)


def kernel(
    cfg,
    ids_ref,
    survive_ref,
    hot_ref,
    table_ref,
    feat_ref,
    sum_ref,
    count_ref,
    hot_sum_ref,
    hot_count_ref,
    bucket,
    arrived,
    hot_part,
    hot_in,
    hot_red,
    hot_all,
    send1,
    recv1,
    send2,
    recv2,
    hsend,
    hrecv,
    gsend,
    grecv,
):
    owners, reps, cap, own_groups, home_dev = cfg
    rows, width = feat_ref.shape
    hots = hot_ref.shape[1]
    nb = width // cap
    chunks = owners // nb
    pieces = hots // reps // SUB
    ndev = owners * reps
    me = lax.axis_index("owner")
    rep = lax.axis_index("rep")
    dev = me * reps + rep

    barrier = pltpu.get_barrier_semaphore()

    @pl.loop(1, ndev)
    def _(d):
        other = lax.rem(dev + d, ndev)
        pl.semaphore_signal(
            barrier, inc=1, device_id=(other // reps, lax.rem(other, reps)), device_id_type=MESH
        )

    ids = ids_ref[...]
    live = survive_ref[...] == 1
    table = table_ref[...]
    trows = table.shape[0]
    halves = jnp.concatenate([table >> 8, table & 255], axis=1).astype(F32).astype(BF)
    pick = jnp.where(iota((trows, rows), 0) == (ids >> 7), 1.0, 0.0).astype(BF)
    both = mm(halves, pick, ((0,), (0,)))
    column = both[:LANES] * 256.0 + both[LANES:]
    home = jnp.sum(
        jnp.where(iota((LANES, rows), 0) == (ids & (LANES - 1)), column, 0.0), axis=0, keepdims=True
    )
    target = jnp.floor(home * (1.0 / own_groups))
    label = home - target * own_groups + 1.0
    ahead = target - me.astype(F32)
    ahead = jnp.where(ahead < 0.0, ahead + owners, ahead)

    hot_col = jnp.sum(
        jnp.where(iota((hots, hots), 0) == iota((hots, hots), 1), hot_ref[...].astype(F32), 0.0),
        axis=1,
        keepdims=True,
    )
    matches = jnp.where(hot_col == ids.astype(F32), 1.0, 0.0)
    is_hot = jnp.max(matches, axis=0, keepdims=True)
    live_f = jnp.where(live, 1.0, 0.0)
    keep = live_f * (1.0 - is_hot)
    ahead = jnp.where(keep > 0.0, ahead, -1.0)
    ahead_i = ahead.astype(jnp.int32)

    member = jnp.where(iota((owners, rows), 0) == ahead_i, 1.0, 0.0)
    before = jnp.where(iota((rows, rows), 0) < iota((rows, rows), 1), 1.0, 0.0).astype(BF)
    position = mm(member.astype(BF), before)
    placed = jnp.sum(position * member, axis=0, keepdims=True)
    slot = jnp.where(keep > 0.0, ahead * cap + placed, -1.0).astype(jnp.int32)
    lane = (placed + cap * (ahead - nb * jnp.floor(ahead * (1.0 / nb)))).astype(jnp.int32)
    label_hi = jnp.floor(label * (1.0 / 256.0))
    label_lo = label - 256.0 * label_hi
    coded = jnp.concatenate([member * label_hi, member * label_lo], axis=0).astype(BF)
    where = jnp.where(iota((width, rows), 0) == lane, 1.0, 0.0).astype(BF)
    coded = mm(coded, where, ((1,), (1,)))
    labels = coded[:owners] * 256.0 + coded[owners:]

    feat_hi, feat_lo = split(feat_ref[...])
    blocks = []
    for c in range(chunks):
        place = jnp.where(iota((width, rows), 0) + c * width == slot, 1.0, 0.0).astype(BF)
        packed = mm(place, feat_hi) + mm(place, feat_lo)
        for i in range(nb):
            k = c * nb + i
            dst = arrived.at[0, 0] if k == 0 else bucket.at[k - 1]
            dst[:cap, :] = packed[i * cap : (i + 1) * cap]
            dst[cap:, :] = jnp.broadcast_to(labels[k : k + 1], (SUB, width))

    pl.semaphore_wait(barrier, ndev - 1)

    def send_block(k):
        return pltpu.make_async_remote_copy(
            src_ref=bucket.at[k - 1],
            dst_ref=arrived.at[0, k],
            send_sem=send1,
            recv_sem=recv1.at[k],
            device_id=(lax.rem(me + k, owners), rep),
            device_id_type=MESH,
        )

    def forward(q, k):
        return pltpu.make_async_remote_copy(
            src_ref=arrived.at[0, k],
            dst_ref=arrived.at[q, k],
            send_sem=send2,
            recv_sem=recv2.at[q, k],
            device_id=(me, lax.rem(rep + q, reps)),
            device_id_type=MESH,
        )

    def forward_all(k):
        for q in range(1, reps):
            forward(q, k).start()

    @pl.loop(1, owners)
    def _(k):
        send_block(k).start()

    forward_all(0)

    hot_table = matches * live_f
    tally = jnp.sum(hot_table, axis=1, keepdims=True)
    hot_bf = hot_table.astype(BF)
    sums = mm(hot_bf, feat_hi) + mm(hot_bf, feat_lo)
    hot_part[:, :, :width] = sums.reshape(hots // SUB, SUB, width)
    hot_part[:, :, width:] = jnp.broadcast_to(tally, (hots, LANES)).reshape(hots // SUB, SUB, LANES)

    def hot_send(b):
        to_owner = lax.rem(b, pieces)
        to_rep = b // pieces
        to = to_owner * reps + to_rep
        back = lax.rem(to - dev + ndev, ndev)
        return to, pltpu.make_async_remote_copy(
            src_ref=hot_part.at[b],
            dst_ref=hot_in.at[back],
            send_sem=hsend.at[b],
            recv_sem=hrecv,
            device_id=(to_owner, to_rep),
            device_id_type=MESH,
        )

    @pl.loop(0, hots // SUB)
    def _(b):
        to, copy = hot_send(b)

        @pl.when(to != dev)
        def _():
            copy.start()

    tiles = max(1, home_dev // 512)
    tile = home_dev // tiles
    base = rep * home_dev + 1
    sum_ref[...] = jnp.zeros_like(sum_ref)
    count_ref[...] = jnp.zeros_like(count_ref)

    def add_chunk(q, c):
        lab = arrived[q, c * nb, cap : cap + SUB, :]
        for i in range(1, nb):
            lab = lab + arrived[q, c * nb + i, cap : cap + SUB, :]
        lab = lab[:1].astype(jnp.int32) - base
        block = jnp.concatenate([arrived[q, c * nb + i, :cap, :] for i in range(nb)], axis=0)
        hi, lo = split(block)
        ones = jnp.ones((SUB, width), BF)

        for t in range(tiles):
            onehot = jnp.where(iota((tile, width), 0) + t * tile == lab, 1.0, 0.0).astype(BF)
            at = pl.ds(t * tile, tile)
            sum_ref[at, :] += mm(onehot, hi) + mm(onehot, lo)
            count_ref[:, at] += mm(ones, onehot, ((1,), (1,)))

    def own_chunk(c):
        @pl.loop(max(1, c * nb), (c + 1) * nb)
        def _(k):
            send_block(k).wait_recv()
            forward_all(k)

        add_chunk(0, c)

    def peer_chunk(c):
        for q in range(1, reps):

            @pl.loop(c * nb, (c + 1) * nb)
            def _(k):
                forward(q, k).wait_recv()

            add_chunk(q, c)

    def hot_gather(d):
        return pltpu.make_async_remote_copy(
            src_ref=hot_red,
            dst_ref=hot_all.at[me],
            send_sem=gsend.at[d],
            recv_sem=grecv.at[me],
            device_id=(lax.rem(me + d, owners), rep),
            device_id_type=MESH,
        )

    own_chunk(0)

    @pl.when(me < pieces)
    def _():
        mine = hot_in.at[pl.ds(1, ndev - 1)]
        pltpu.make_async_copy(mine, mine, hrecv).wait()
        total = hot_part[rep * pieces + me] + jnp.sum(hot_in[1:], axis=0)
        hot_red[...] = total
        hot_all[me] = total

        @pl.loop(1, owners)
        def _(d):
            hot_gather(d).start()

    for c in range(1, chunks):
        own_chunk(c)
        peer_chunk(c - 1)
    peer_chunk(chunks - 1)

    @pl.loop(0, pieces)
    def _(p):
        @pl.when(p != me)
        def _():
            pltpu.make_async_copy(hot_all.at[p], hot_all.at[p], grecv.at[p]).wait()

    per_rep = pieces * SUB
    everything = hot_all[...].reshape(per_rep, width + LANES)
    hot_sum_ref[...] = everything[:, :width]
    counts = everything[:, width:]
    diagonal = jnp.where(iota((per_rep, LANES), 0) == iota((per_rep, LANES), 1), counts, 0.0)
    hot_count_ref[...] = jnp.broadcast_to(jnp.sum(diagonal, axis=0, keepdims=True), (SUB, LANES))

    @pl.when(me < pieces)
    def _():
        @pl.loop(1, owners)
        def _(d):
            hot_gather(d).wait_send()

    @pl.loop(0, hots // SUB)
    def _(b):
        to, copy = hot_send(b)

        @pl.when(to != dev)
        def _():
            copy.wait_send()

    pltpu.make_async_copy(bucket, bucket, send1).wait()
    if reps > 1:
        sent = arrived.at[pl.ds(1, reps - 1)]
        pltpu.make_async_copy(sent, sent, send2).wait()


def local(features, group_ids, survive, home_row, hot_ids):
    rows, width = features.shape
    owners = lax.axis_size("owner")
    reps = lax.axis_size("rep")
    groups = home_row.shape[0]
    hots = hot_ids.shape[0]
    own_groups = groups // owners
    home_dev = own_groups // reps
    cap = 2 * rows // owners
    pieces = hots // reps // SUB
    cfg = (owners, reps, cap, own_groups, home_dev)
    vmem = pl.BlockSpec(memory_space=pltpu.VMEM)
    DMA = pltpu.SemaphoreType.DMA
    cold_sum, count, hot_sum, hot_count = pl.pallas_call(
        functools.partial(kernel, cfg),
        out_shape=(
            jax.ShapeDtypeStruct((home_dev, width), F32),
            jax.ShapeDtypeStruct((SUB, home_dev), F32),
            jax.ShapeDtypeStruct((hots // reps, width), F32),
            jax.ShapeDtypeStruct((SUB, LANES), F32),
        ),
        in_specs=[vmem] * 5,
        out_specs=[vmem] * 4,
        scratch_shapes=[
            pltpu.VMEM((owners - 1, cap + SUB, width), F32),
            pltpu.VMEM((reps, owners, cap + SUB, width), F32),
            pltpu.VMEM((hots // SUB, SUB, width + LANES), F32),
            pltpu.VMEM((owners * reps, SUB, width + LANES), F32),
            pltpu.VMEM((SUB, width + LANES), F32),
            pltpu.VMEM((pieces, SUB, width + LANES), F32),
            DMA(()),
            DMA((owners,)),
            DMA(()),
            DMA((reps, owners)),
            DMA((hots // SUB,)),
            DMA(()),
            DMA((owners,)),
            DMA((pieces,)),
        ],
        compiler_params=pltpu.CompilerParams(
            collective_id=0, has_side_effects=True, vmem_limit_bytes=48 << 20
        ),
    )(
        group_ids.reshape(1, rows),
        survive.reshape(1, rows),
        hot_ids.reshape(1, hots),
        home_row.reshape(groups // LANES, LANES),
        features,
    )
    group_count = count[0]
    counts_hot = hot_count[0, : hots // reps]
    group_out = cold_sum / jnp.sqrt(1.0 + group_count)[:, None]
    hot_out = hot_sum / jnp.sqrt(1.0 + counts_hot)[:, None]
    return group_out, group_count, hot_out, counts_hot


def solution(mesh):
    in_specs = (P(("owner", "rep"), None), P(("owner", "rep")), P(("owner", "rep")), P(), P())
    out_specs = (P(("owner", "rep"), None), P(("owner", "rep")), P("rep", None), P("rep"))
    return jax.shard_map(local, mesh=mesh, in_specs=in_specs, out_specs=out_specs, check_vma=False)
```

time: 346 us -> 73.1 us (0.21); the launches traced: 342 us -> 72.8 us
  local copies, waits for them, and re-layouts: 141 us -> 4.03 us
  waiting for transfers between devices: 95.2 us -> 0 us
  Pallas kernels: 0 us -> 65.2 us
  blocking collectives: 40.7 us -> 0 us
  matrix products: 20.1 us -> 0 us
  starting transfers between devices: 15.6 us -> 0 us
  between operations: 15.2 us -> 0.66 us
  other arithmetic: 13.5 us -> 2.93 us
    scatter x2 -> x0, local copies, waits for them, and re-layouts: 135 us -> none  [the longest x1 72.8 us: local(): labels = jnp.full((owners, capacity), -1.0, jnp.float32).at[target_safe,...]
    reduce_scatter x2 -> x0, waiting for transfers between devices: 70.2 us -> none  [the longest x1 56.6 us: local(): lax.psum_scatter(dense, 'rep', scatter_dimension=0, tiled=True)]
    pallas_call x0 -> x1, Pallas kernels: none -> 65.2 us  [local(): pl.pallas_call(functools.partial(kernel, cfg), out_shape=(jax.ShapeDtypeS...]
    psum x1 -> x0, blocking collectives: 33.1 us -> none  [local(): hot_sum, hot_count = lax.psum((part_sum, part_tally), 'owner')]
    dot_general x3 -> x0, matrix products: 20.1 us -> none  [the longest x2 18.5 us: add_block(): lax.dot_general(onehot, block_rows, (((0,), (0,)), ((), ())), precision=l...]
    psum x1 -> x0, waiting for transfers between devices: 17.7 us -> none  [local(): hot_sum, hot_count = lax.psum((part_sum, part_tally), 'owner')]
    all_to_all x2 -> x0, starting transfers between devices: 15.5 us -> none  [the longest x1 9.47 us: local(): lax.all_to_all(labels, 'owner', split_axis=0, concat_axis=0, tiled=True)]
    unnamed x1 -> x0, blocking collectives: 7.62 us -> none
  transfers between devices with their start and end apart: 5 -> 0, of which waited for: 4 -> 0; matrix products, arithmetic and copies ran while one was open for 27% -> 0% of each run, Pallas kernels for 0% -> 0%
where the time goes in v1:
time: 73.1 us; the launch traced here: 72.8 us
  Pallas kernels  65.2 us (89%)
  local copies, waits for them, and re-layouts  4.03 us (6%)
  other arithmetic  2.93 us (4%)
    pallas_call x1, Pallas kernels, local(): pl.pallas_call(functools.partial(kernel, cfg), out_shape=(jax.ShapeDtypeS...  65.2 us
    unnamed x12, local copies, waits for them, and re-layouts  4.03 us
    div x1, other arithmetic, local(): group_out = cold_sum / jnp.sqrt(1.0 + group_count)[:, None]  1.67 us

profile of v1, /device:TPU:0, one launch (start us, length us, event | category | flops | bytes accessed | tf_op | source)
XLA Modules:
  0.0 72.8 jit_solution(10618835115214164685)
XLA Ops:
  0.6 0.0 copy-start
  0.6 1.0 %copy-done = f32[512,256]{1,0:T(8,128)S(1)} copy-done((f32[512,256]{1,0:T(8,128)S(1)}, f32[512,256]{1,0:T(8,128)}, u32[]{:S(2)}) %copy-start) | copy-done | bytes 524312
  1.7 0.0 copy-start.1
  1.7 0.9 %copy-done.1 = s32[65536]{0:T(1024)S(1)} copy-done((s32[65536]{0:T(1024)S(1)}, s32[65536]{0:T(1024)}, u32[]{:S(2)}) %copy-start.1) | copy-done | bytes 262168
  2.6 0.0 copy-start.2
  2.6 0.7 copy-done.2
  3.3 0.0 copy-start.3
  3.3 0.7 copy-done.3
  4.0 0.0 copy-start.4
  4.0 0.7 copy-done.4
  4.7 65.2 %shard_map.84 = (f32[2048,256]{1,0:T(8,128)S(1)}, f32[8,2048]{1,0:T(8,128)S(1)}, f32[128,256]{1,0:T(8,128)S(1)}, f32[8,128]{1,0:T(8,128)S(1)}) custom-call(s32[1,512]{1,0:T(1,128)S(1)} %bitcast.9, s32[1,512]{1,0:T(1,128)S(1)} %bitcast.10, s32[1,256]{1,0:T(1,128)S(1)} %bitcast.11, s32[512,128]{1,0:T(8,128)S(1)} %bitcast.8, f32[512,256]{1,0:T(8,128)S(1)} %copy-done), custom_call_target="tpu_custom_call" | custom-call | tf_op jit(solution)/shard_map/pallas_call | solution.py:302
  69.9 0.5 add_sqrt_fusion.1
  70.4 0.7 %broadcast_divide_fusion.1 = f32[128,256]{1,0:T(8,128)} fusion(f32[128,256]{1,0:T(8,128)S(1)} %get-tuple-element.10, f32[128]{0:T(128)S(1)} %get-tuple-element.12), kind=kLoop, calls=%fused_computation.1 | loop fusion | flops 32768 | bytes 262656 | tf_op jit(solution)/shard_map/div | solution.py:341
  71.1 0.0 copy-start.5
  71.1 1.7 %broadcast_divide_fusion = f32[2048,256]{1,0:T(8,128)} fusion(f32[2048,256]{1,0:T(8,128)S(1)} %get-tuple-element.8, f32[2048]{0:T(1024)S(1)} %add_sqrt_fusion), kind=kLoop, calls=%fused_computation | loop fusion | flops 524288 | bytes 4202496 | tf_op jit(solution)/shard_map/div | solution.py:340
  72.8 0.0 copy-done.5
  (2 shorter events, 0.0 us)
Async XLA Ops:
  0.6 1.0 %copy-start = (f32[512,256]{1,0:T(8,128)S(1)}, f32[512,256]{1,0:T(8,128)}, u32[]{:S(2)}) copy-start(f32[512,256]{1,0:T(8,128)} %feat_ref.1) | copy-start | bytes 1572868
  1.7 0.9 %copy-start.1 = (s32[65536]{0:T(1024)S(1)}, s32[65536]{0:T(1024)}, u32[]{:S(2)}) copy-start(s32[65536]{0:T(1024)} %param.8) | copy-start | bytes 786436
  2.6 0.7 copy-start.2
  3.3 0.7 copy-start.3
  4.0 0.7 copy-start.4
  71.1 1.7 %copy-start.5 = (f32[1,2048]{1,0:T(1,128)}, f32[1,2048]{1,0:T(1,128)S(1)}, u32[]{:S(2)}) copy-start(f32[1,2048]{1,0:T(1,128)S(1)} %slice.6) | copy-start | bytes 24580

commit v2 on v1

v2 whole, which is shorter than its diff:
```python
import functools

import jax
import jax.numpy as jnp
from jax import lax
from jax.experimental import pallas as pl
from jax.experimental.pallas import tpu as pltpu
from jax.sharding import PartitionSpec as P

MESH = pl.DeviceIdType.MESH
LANES = 128
SUB = 8
BF = jnp.bfloat16
F32 = jnp.float32


def iota(shape, axis):
    return lax.broadcasted_iota(jnp.int32, shape, axis)


def mm(a, b, dims=((1,), (0,))):
    return lax.dot_general(a, b, (dims, ((), ())), preferred_element_type=F32)


def split(x):
    hi = x.astype(BF)
    return hi, (x - hi.astype(F32)).astype(BF)


def kernel(
    cfg,
    ids_hbm,
    survive_hbm,
    hot_hbm,
    table_hbm,
    feat_hbm,
    sum_ref,
    count_ref,
    hot_sum_ref,
    hot_count_ref,
    ids_ref,
    survive_ref,
    hot_ref,
    table_ref,
    feat_ref,
    bucket,
    arrived,
    tags,
    tags_in,
    hot_part,
    hot_l1,
    hot_s1,
    hot_l2,
    hot_s2,
    hot_l3,
    hot_red,
    hot_all,
    load,
    send1,
    recv1,
    send2,
    recv2,
    tsend,
    trecv,
    s_core,
    r_core,
    s_rep,
    r_rep,
    s_chip,
    r_chip,
    s_all,
    r_all,
    s_last,
    r_last,
):
    owners, reps, cap, own_groups, home_dev = cfg
    rows, width = feat_ref.shape
    hots = hot_ref.shape[1]
    nb = width // cap
    chunks = owners // nb
    chips = owners // 2
    pieces = hots // reps // 2 // SUB
    part = pieces * SUB
    ndev = owners * reps
    half = owners // 2
    quarter = owners // 4
    me = lax.axis_index("owner")
    rep = lax.axis_index("rep")
    dev = me * reps + rep
    core = lax.rem(me, 2)
    chip = me // 2

    loads = [
        pltpu.make_async_copy(src, dst, load.at[i])
        for i, (src, dst) in enumerate(
            (
                (table_hbm, table_ref),
                (ids_hbm, ids_ref),
                (survive_hbm, survive_ref),
                (hot_hbm, hot_ref),
                (feat_hbm, feat_ref),
            )
        )
    ]
    for copy in loads:
        copy.start()

    barrier = pltpu.get_barrier_semaphore()

    @pl.loop(1, ndev)
    def _(d):
        other = lax.rem(dev + d, ndev)
        pl.semaphore_signal(
            barrier, inc=1, device_id=(other // reps, lax.rem(other, reps)), device_id_type=MESH
        )

    flips = []
    bit = 1
    while bit < owners:
        flips.append((bit, bit - 2 * bit * lax.rem(me // bit, 2)))
        bit *= 2

    def partner(p):
        v = p - half
        number = p if p < half else half + v // 2 + (v % 2) * quarter
        out = me
        for bit, flip in flips:
            if number & bit:
                out = out + flip
        return out

    for copy in loads[:4]:
        copy.wait()
    ids = ids_ref[...]
    live_f = jnp.where(survive_ref[...] == 1, 1.0, 0.0)
    table = table_ref[...]
    trows = table.shape[0]
    halves = jnp.concatenate([table >> 8, table & 255], axis=1).astype(F32).astype(BF)
    pick = jnp.where(iota((trows, rows), 0) == (ids >> 7), 1.0, 0.0).astype(BF)
    both = mm(halves, pick, ((0,), (0,)))
    column = both[:LANES] * 256.0 + both[LANES:]
    home = jnp.sum(
        jnp.where(iota((LANES, rows), 0) == (ids & (LANES - 1)), column, 0.0), axis=0, keepdims=True
    )
    target = jnp.floor(home * (1.0 / own_groups))
    label = home - target * own_groups + 1.0
    number = target.astype(jnp.int32) ^ me
    low = number & (half - 1)
    spread = half + 2 * (low & (quarter - 1)) + jnp.where(low >= quarter, 1, 0)
    place_at = jnp.where(number < half, number, spread)

    hot_col = jnp.sum(
        jnp.where(iota((hots, hots), 0) == iota((hots, hots), 1), hot_ref[...].astype(F32), 0.0),
        axis=1,
        keepdims=True,
    )
    matches = jnp.where(hot_col == ids.astype(F32), 1.0, 0.0)
    is_hot = jnp.max(matches, axis=0, keepdims=True)
    keep = live_f * (1.0 - is_hot)
    place_at = jnp.where(keep > 0.0, place_at, -1)

    member = jnp.where(iota((owners, rows), 0) == place_at, 1.0, 0.0)
    before = jnp.where(iota((rows, rows), 0) < iota((rows, rows), 1), 1.0, 0.0).astype(BF)
    position = mm(member.astype(BF), before)
    placed = jnp.sum(position * member, axis=0, keepdims=True).astype(jnp.int32)
    slot = jnp.where(keep > 0.0, place_at * cap + placed, -1)
    lane = placed + cap * (place_at & (nb - 1))
    label_hi = jnp.floor(label * (1.0 / 256.0))
    label_lo = label - 256.0 * label_hi
    coded = jnp.concatenate([member * label_hi, member * label_lo], axis=0).astype(BF)
    where = jnp.where(iota((width, rows), 0) == lane, 1.0, 0.0).astype(BF)
    coded = mm(coded, where, ((1,), (1,)))
    labels = coded[:owners] * 256.0 + coded[owners:]
    for p in range(owners):
        tags[p] = labels[p : p + 1]

    def send_block(p):
        return pltpu.make_async_remote_copy(
            src_ref=bucket.at[p - 1],
            dst_ref=arrived.at[0, p],
            send_sem=send1,
            recv_sem=recv1.at[p],
            device_id=(partner(p), rep),
            device_id_type=MESH,
        )

    def send_tag(q, p):
        return pltpu.make_async_remote_copy(
            src_ref=tags.at[p],
            dst_ref=tags_in.at[q, p],
            send_sem=tsend.at[q, p],
            recv_sem=trecv.at[q, p],
            device_id=(partner(p), lax.rem(rep + q, reps)),
            device_id_type=MESH,
        )

    def forward(q, p):
        return pltpu.make_async_remote_copy(
            src_ref=arrived.at[0, p],
            dst_ref=arrived.at[q, p],
            send_sem=send2,
            recv_sem=recv2.at[q, p],
            device_id=(me, lax.rem(rep + q, reps)),
            device_id_type=MESH,
        )

    pairs = [(q, p) for p in range(owners) for q in range(reps) if q + p]
    tags_in[0, 0] = labels[:1]
    loads[4].wait()
    feat_hi, feat_lo = split(feat_ref[...])
    for c in range(chunks):
        place = jnp.where(iota((width, rows), 0) + c * width == slot, 1.0, 0.0).astype(BF)
        packed = mm(place, feat_hi) + mm(place, feat_lo)
        for i in range(nb):
            p = c * nb + i
            dst = arrived.at[0, 0] if p == 0 else bucket.at[p - 1]
            dst[...] = packed[i * cap : (i + 1) * cap]
        if c == 0:
            pl.semaphore_wait(barrier, ndev - 1)
        for p in range(c * nb, (c + 1) * nb):
            if p == 0:
                for q in range(1, reps):
                    forward(q, 0).start()
            else:
                send_block(p).start()
    for q, p in pairs:
        send_tag(q, p).start()

    hot_table = matches * live_f
    tally = jnp.sum(hot_table, axis=1, keepdims=True)
    hot_bf = hot_table.astype(BF)
    sums = mm(hot_bf, feat_hi) + mm(hot_bf, feat_lo)
    hot_part[:, :, :, :width] = sums.reshape(reps, 2, part, width)
    hot_part[:, :, :, width:] = jnp.broadcast_to(tally, (hots, LANES)).reshape(reps, 2, part, LANES)
    mate = (me + 1 - 2 * core, rep)
    to_core = pltpu.make_async_remote_copy(
        src_ref=hot_part.at[:, 1 - core],
        dst_ref=hot_l1,
        send_sem=s_core,
        recv_sem=r_core,
        device_id=mate,
        device_id_type=MESH,
    )
    to_core.start()

    def to_rep(q):
        other = lax.rem(rep + q, reps)
        return pltpu.make_async_remote_copy(
            src_ref=hot_s1.at[other],
            dst_ref=hot_l2.at[q],
            send_sem=s_rep.at[q],
            recv_sem=r_rep.at[q],
            device_id=(me, other),
            device_id_type=MESH,
        )

    def to_chip(p):
        return pltpu.make_async_remote_copy(
            src_ref=hot_s2.at[p],
            dst_ref=hot_l3.at[lax.rem(p - chip + chips, chips)],
            send_sem=s_chip.at[p],
            recv_sem=r_chip,
            device_id=(p * 2 + core, rep),
            device_id_type=MESH,
        )

    def to_all(d):
        return pltpu.make_async_remote_copy(
            src_ref=hot_red,
            dst_ref=hot_all.at[core, chip],
            send_sem=s_all.at[d],
            recv_sem=r_all.at[chip],
            device_id=(lax.rem(chip + d, chips) * 2 + core, rep),
            device_id_type=MESH,
        )

    to_mate = pltpu.make_async_remote_copy(
        src_ref=hot_all.at[core],
        dst_ref=hot_all.at[core],
        send_sem=s_last,
        recv_sem=r_last,
        device_id=mate,
        device_id_type=MESH,
    )

    def hot_step_1():
        to_core.wait_recv()
        hot_s1[...] = hot_part[:, core] + hot_l1[...]
        for q in range(1, reps):
            to_rep(q).start()

    def hot_step_2():
        total = hot_s1[rep]
        for q in range(1, reps):
            to_rep(q).wait_recv()
            total = total + hot_l2[q]
        hot_s2[...] = total.reshape(pieces, SUB, width + LANES)

        @pl.loop(0, pieces)
        def _(p):
            @pl.when(p != chip)
            def _():
                to_chip(p).start()

    def hot_step_3():
        @pl.when(chip < pieces)
        def _():
            mine = hot_l3.at[pl.ds(1, chips - 1)]
            pltpu.make_async_copy(mine, mine, r_chip).wait()
            total = hot_s2[chip] + jnp.sum(hot_l3[1:], axis=0)
            hot_red[...] = total
            hot_all[core, chip] = total

            @pl.loop(1, chips)
            def _(d):
                to_all(d).start()

    def hot_step_4():
        @pl.loop(0, pieces)
        def _(p):
            @pl.when(p != chip)
            def _():
                pltpu.make_async_copy(hot_all.at[core, p], hot_all.at[core, p], r_all.at[p]).wait()

        to_mate.start()

    def hot_step_5():
        to_mate.wait_recv()
        everything = hot_all[...].reshape(2 * part, width + LANES)
        hot_sum_ref[...] = everything[:, :width]
        counts = everything[:, width:]
        diagonal = jnp.where(iota((2 * part, LANES), 0) == iota((2 * part, LANES), 1), counts, 0.0)
        hot_count_ref[...] = jnp.broadcast_to(jnp.sum(diagonal, axis=0, keepdims=True), (SUB, LANES))

    tiles = max(1, home_dev // 512)
    tile = home_dev // tiles
    base = rep * home_dev + 1

    def add_chunk(q, c):
        first = q == 0 and c == 0
        lab = jnp.zeros((1, width), F32)
        for p in range(c * nb, (c + 1) * nb):
            if q + p:
                send_tag(q, p).wait_recv()
            lab = lab + tags_in[q, p]
        lab = lab.astype(jnp.int32) - base
        block = jnp.concatenate([arrived[q, c * nb + i] for i in range(nb)], axis=0)
        hi, lo = split(block)
        ones = jnp.ones((SUB, width), BF)

        for t in range(tiles):
            onehot = jnp.where(iota((tile, width), 0) + t * tile == lab, 1.0, 0.0).astype(BF)
            at = pl.ds(t * tile, tile)
            total = mm(onehot, hi) + mm(onehot, lo)
            tally = mm(ones, onehot, ((1,), (1,)))
            if first:
                sum_ref[at, :] = total
                count_ref[:, at] = tally
            else:
                sum_ref[at, :] += total
                count_ref[:, at] += tally

    def pass_on(c):
        for p in range(max(1, c * nb), (c + 1) * nb):
            send_block(p).wait_recv()
            for q in range(1, reps):
                forward(q, p).start()

    def peer_chunk(c):
        for q in range(1, reps):
            for p in range(c * nb, (c + 1) * nb):
                forward(q, p).wait_recv()
            add_chunk(q, c)

    steps = [hot_step_1, hot_step_2, hot_step_3]
    for c in range(chunks):
        pass_on(c)
        if steps:
            steps.pop(0)()
        add_chunk(0, c)
        if c:
            peer_chunk(c - 1)
    for step in steps:
        step()
    hot_step_4()
    hot_step_5()
    peer_chunk(chunks - 1)

    to_core.wait_send()
    for q in range(1, reps):
        to_rep(q).wait_send()

    @pl.loop(0, pieces)
    def _(p):
        @pl.when(p != chip)
        def _():
            to_chip(p).wait_send()

    @pl.when(chip < pieces)
    def _():
        @pl.loop(1, chips)
        def _(d):
            to_all(d).wait_send()

    to_mate.wait_send()
    for q, p in pairs:
        send_tag(q, p).wait_send()
    pltpu.make_async_copy(bucket, bucket, send1).wait()
    if reps > 1:
        sent = arrived.at[pl.ds(1, reps - 1)]
        pltpu.make_async_copy(sent, sent, send2).wait()


def local(features, group_ids, survive, home_row, hot_ids):
    rows, width = features.shape
    owners = lax.axis_size("owner")
    reps = lax.axis_size("rep")
    groups = home_row.shape[0]
    hots = hot_ids.shape[0]
    own_groups = groups // owners
    home_dev = own_groups // reps
    cap = 2 * rows // owners
    chips = owners // 2
    pieces = hots // reps // 2 // SUB
    part = pieces * SUB
    wide = width + LANES
    cfg = (owners, reps, cap, own_groups, home_dev)
    vmem = pl.BlockSpec(memory_space=pltpu.VMEM)
    hbm = pl.BlockSpec(memory_space=pltpu.HBM)
    DMA = pltpu.SemaphoreType.DMA
    VM = pltpu.VMEM
    cold_sum, count, hot_sum, hot_count = pl.pallas_call(
        functools.partial(kernel, cfg),
        out_shape=(
            jax.ShapeDtypeStruct((home_dev, width), F32),
            jax.ShapeDtypeStruct((SUB, home_dev), F32),
            jax.ShapeDtypeStruct((hots // reps, width), F32),
            jax.ShapeDtypeStruct((SUB, LANES), F32),
        ),
        in_specs=[hbm] * 5,
        out_specs=[vmem] * 4,
        scratch_shapes=[
            VM((1, rows), jnp.int32),
            VM((1, rows), jnp.int32),
            VM((1, hots), jnp.int32),
            VM((groups // LANES, LANES), jnp.int32),
            VM((rows, width), F32),
            VM((owners - 1, cap, width), F32),
            VM((reps, owners, cap, width), F32),
            VM((owners, 1, width), F32),
            VM((reps, owners, 1, width), F32),
            VM((reps, 2, part, wide), F32),
            VM((reps, part, wide), F32),
            VM((reps, part, wide), F32),
            VM((reps, part, wide), F32),
            VM((pieces, SUB, wide), F32),
            VM((chips, SUB, wide), F32),
            VM((SUB, wide), F32),
            VM((2, pieces, SUB, wide), F32),
            DMA((5,)),
            DMA(()),
            DMA((owners,)),
            DMA(()),
            DMA((reps, owners)),
            DMA((reps, owners)),
            DMA((reps, owners)),
            DMA(()),
            DMA(()),
            DMA((reps,)),
            DMA((reps,)),
            DMA((pieces,)),
            DMA(()),
            DMA((chips,)),
            DMA((pieces,)),
            DMA(()),
            DMA(()),
        ],
        compiler_params=pltpu.CompilerParams(
            collective_id=0, has_side_effects=True, vmem_limit_bytes=48 << 20
        ),
    )(
        group_ids.reshape(1, rows),
        survive.reshape(1, rows),
        hot_ids.reshape(1, hots),
        home_row.reshape(groups // LANES, LANES),
        features,
    )
    group_count = count[0]
    counts_hot = hot_count[0, : hots // reps]
    group_out = cold_sum / jnp.sqrt(1.0 + group_count)[:, None]
    hot_out = hot_sum / jnp.sqrt(1.0 + counts_hot)[:, None]
    return group_out, group_count, hot_out, counts_hot


def solution(mesh):
    in_specs = (P(("owner", "rep"), None), P(("owner", "rep")), P(("owner", "rep")), P(), P())
    out_specs = (P(("owner", "rep"), None), P(("owner", "rep")), P("rep", None), P("rep"))
    return jax.shard_map(local, mesh=mesh, in_specs=in_specs, out_specs=out_specs, check_vma=False)
```

time: 73.1 us -> 53.3 us (0.73)
  Pallas kernels: 65.2 us -> 45.4 us
    pallas_call x1, Pallas kernels: 65.2 us -> 45.4 us  [local(): pl.pallas_call(functools.partial(kernel, cfg), out_shape=(jax.ShapeDtypeS...]
where the time goes in v2:
time: 53.3 us; the launch traced here: 53 us
  Pallas kernels  45.4 us (85%)
  local copies, waits for them, and re-layouts  4.03 us (8%)
  other arithmetic  2.93 us (5%)
  between operations  0.66 us (1%)
    pallas_call x1, Pallas kernels, local(): pl.pallas_call(functools.partial(kernel, cfg), out_shape=(jax.ShapeDtypeS...  45.4 us
    unnamed x12, local copies, waits for them, and re-layouts  4.03 us
    div x1, other arithmetic, local(): group_out = cold_sum / jnp.sqrt(1.0 + group_count)[:, None]  1.67 us

profile of v2, /device:TPU:0, one launch (start us, length us, event | category | flops | bytes accessed | tf_op | source)
XLA Modules:
  0.0 53.0 jit_solution(1821064861059168622)
XLA Ops:
  0.6 0.0 copy-start
  0.6 1.0 %copy-done = f32[512,256]{1,0:T(8,128)S(1)} copy-done((f32[512,256]{1,0:T(8,128)S(1)}, f32[512,256]{1,0:T(8,128)}, u32[]{:S(2)}) %copy-start) | copy-done | bytes 524312
  1.7 0.0 copy-start.1
  1.7 0.9 %copy-done.1 = s32[65536]{0:T(1024)S(1)} copy-done((s32[65536]{0:T(1024)S(1)}, s32[65536]{0:T(1024)}, u32[]{:S(2)}) %copy-start.1) | copy-done | bytes 262168
  2.6 0.0 copy-start.2
  2.6 0.7 %copy-done.2 = s32[512]{0:T(512)S(1)} copy-done((s32[512]{0:T(512)S(1)}, s32[512]{0:T(512)}, u32[]{:S(2)}) %copy-start.2) | copy-done | bytes 2072
  3.3 0.0 copy-start.3
  3.3 0.7 %copy-done.3 = s32[512]{0:T(512)S(1)} copy-done((s32[512]{0:T(512)S(1)}, s32[512]{0:T(512)}, u32[]{:S(2)}) %copy-start.3) | copy-done | bytes 2072
  4.0 0.0 copy-start.4
  4.0 0.7 %copy-done.4 = s32[256]{0:T(256)S(1)} copy-done((s32[256]{0:T(256)S(1)}, s32[256]{0:T(256)}, u32[]{:S(2)}) %copy-start.4) | copy-done | bytes 1048
  4.7 45.4 %shard_map.84 = (f32[2048,256]{1,0:T(8,128)S(1)}, f32[8,2048]{1,0:T(8,128)S(1)}, f32[128,256]{1,0:T(8,128)S(1)}, f32[8,128]{1,0:T(8,128)S(1)}) custom-call(s32[1,512]{1,0:T(1,128)S(1)} %bitcast.9, s32[1,512]{1,0:T(1,128)S(1)} %bitcast.10, s32[1,256]{1,0:T(1,128)S(1)} %bitcast.11, s32[512,128]{1,0:T(8,128)S(1)} %bitcast.8, f32[512,256]{1,0:T(8,128)S(1)} %copy-done), custom_call_target="tpu_custom_call" | custom-call | tf_op jit(solution)/shard_map/pallas_call | solution.py:432
  50.1 0.5 add_sqrt_fusion.1
  50.6 0.7 %broadcast_divide_fusion.1 = f32[128,256]{1,0:T(8,128)} fusion(f32[128,256]{1,0:T(8,128)S(1)} %get-tuple-element.10, f32[128]{0:T(128)S(1)} %get-tuple-element.12), kind=kLoop, calls=%fused_computation.1 | loop fusion | flops 32768 | bytes 262656 | tf_op jit(solution)/shard_map/div | solution.py:491
  51.3 0.0 copy-start.5
  51.4 1.7 %broadcast_divide_fusion = f32[2048,256]{1,0:T(8,128)} fusion(f32[2048,256]{1,0:T(8,128)S(1)} %get-tuple-element.8, f32[2048]{0:T(1024)S(1)} %add_sqrt_fusion), kind=kLoop, calls=%fused_computation | loop fusion | flops 524288 | bytes 4202496 | tf_op jit(solution)/shard_map/div | solution.py:490
  53.0 0.0 copy-done.5
  (2 shorter events, 0.0 us)
Async XLA Ops:
  0.6 1.0 %copy-start = (f32[512,256]{1,0:T(8,128)S(1)}, f32[512,256]{1,0:T(8,128)}, u32[]{:S(2)}) copy-start(f32[512,256]{1,0:T(8,128)} %feat_hbm.1) | copy-start | bytes 1572868
  1.7 0.9 %copy-start.1 = (s32[65536]{0:T(1024)S(1)}, s32[65536]{0:T(1024)}, u32[]{:S(2)}) copy-start(s32[65536]{0:T(1024)} %param.8) | copy-start | bytes 786436
  2.6 0.7 %copy-start.2 = (s32[512]{0:T(512)S(1)}, s32[512]{0:T(512)}, u32[]{:S(2)}) copy-start(s32[512]{0:T(512)} %param.6) | copy-start | bytes 6148
  3.3 0.7 %copy-start.3 = (s32[512]{0:T(512)S(1)}, s32[512]{0:T(512)}, u32[]{:S(2)}) copy-start(s32[512]{0:T(512)} %param.7) | copy-start | bytes 6148
  4.0 0.7 %copy-start.4 = (s32[256]{0:T(256)S(1)}, s32[256]{0:T(256)}, u32[]{:S(2)}) copy-start(s32[256]{0:T(256)} %param.9) | copy-start | bytes 3076
  51.3 1.7 %copy-start.5 = (f32[1,2048]{1,0:T(1,128)}, f32[1,2048]{1,0:T(1,128)S(1)}, u32[]{:S(2)}) copy-start(f32[1,2048]{1,0:T(1,128)S(1)} %slice.6) | copy-start | bytes 24580

commit v3 on v2

--- a/solution.py
+++ b/solution.py
@@ -208,6 +208,24 @@
     tags_in[0, 0] = labels[:1]
     loads[4].wait()
     feat_hi, feat_lo = split(feat_ref[...])
+    mate = (me + 1 - 2 * core, rep)
+    to_core = pltpu.make_async_remote_copy(
+        src_ref=hot_part.at[:, 1 - core],
+        dst_ref=hot_l1,
+        send_sem=s_core,
+        recv_sem=r_core,
+        device_id=mate,
+        device_id_type=MESH,
+    )
+    def hot_start():
+        hot_table = matches * live_f
+        tally = jnp.sum(hot_table, axis=1, keepdims=True)
+        hot_bf = hot_table.astype(BF)
+        sums = mm(hot_bf, feat_hi) + mm(hot_bf, feat_lo)
+        hot_part[:, :, :, :width] = sums.reshape(reps, 2, part, width)
+        hot_part[:, :, :, width:] = jnp.broadcast_to(tally, (hots, LANES)).reshape(reps, 2, part, LANES)
+        to_core.start()
+
     for c in range(chunks):
         place = jnp.where(iota((width, rows), 0) + c * width == slot, 1.0, 0.0).astype(BF)
         packed = mm(place, feat_hi) + mm(place, feat_lo)
@@ -221,27 +239,12 @@
             if p == 0:
                 for q in range(1, reps):
                     forward(q, 0).start()
-            else:
+            elif c < chunks - 1:
                 send_block(p).start()
+        if c == chunks - 2:
+            hot_start()
     for q, p in pairs:
         send_tag(q, p).start()
-
-    hot_table = matches * live_f
-    tally = jnp.sum(hot_table, axis=1, keepdims=True)
-    hot_bf = hot_table.astype(BF)
-    sums = mm(hot_bf, feat_hi) + mm(hot_bf, feat_lo)
-    hot_part[:, :, :, :width] = sums.reshape(reps, 2, part, width)
-    hot_part[:, :, :, width:] = jnp.broadcast_to(tally, (hots, LANES)).reshape(reps, 2, part, LANES)
-    mate = (me + 1 - 2 * core, rep)
-    to_core = pltpu.make_async_remote_copy(
-        src_ref=hot_part.at[:, 1 - core],
-        dst_ref=hot_l1,
-        send_sem=s_core,
-        recv_sem=r_core,
-        device_id=mate,
-        device_id_type=MESH,
-    )
-    to_core.start()
 
     def to_rep(q):
         other = lax.rem(rep + q, reps)
@@ -372,17 +375,23 @@
                 forward(q, p).wait_recv()
             add_chunk(q, c)
 
-    steps = [hot_step_1, hot_step_2, hot_step_3]
-    for c in range(chunks):
+    hot_step_1()
+    pass_on(0)
+    add_chunk(0, 0)
+    hot_step_2()
+    for p in range((chunks - 1) * nb, owners):
+        send_block(p).start()
+    for c in range(1, chunks - 1):
         pass_on(c)
-        if steps:
-            steps.pop(0)()
+        if c < chunks - 2:
+            add_chunk(0, c)
+    hot_step_3()
+    pass_on(chunks - 1)
+    for c in range(chunks - 2, chunks):
         add_chunk(0, c)
-        if c:
-            peer_chunk(c - 1)
-    for step in steps:
-        step()
     hot_step_4()
+    for c in range(chunks - 1):
+        peer_chunk(c)
     hot_step_5()
     peer_chunk(chunks - 1)
 

time: 53.3 us -> 49.8 us (0.934)
  Pallas kernels: 45.4 us -> 41.9 us
    pallas_call x1, Pallas kernels: 45.4 us -> 41.9 us  [local(): pl.pallas_call(functools.partial(kernel, cfg), out_shape=(jax.ShapeDtypeS...]
where the time goes in v3:
time: 49.8 us; the launch traced here: 49.5 us
  Pallas kernels  41.9 us (84%)
  local copies, waits for them, and re-layouts  4.03 us (8%)
  other arithmetic  2.93 us (6%)
  between operations  0.66 us (1%)
    pallas_call x1, Pallas kernels, local(): pl.pallas_call(functools.partial(kernel, cfg), out_shape=(jax.ShapeDtypeS...  41.9 us
    unnamed x12, local copies, waits for them, and re-layouts  4.03 us
    div x1, other arithmetic, local(): group_out = cold_sum / jnp.sqrt(1.0 + group_count)[:, None]  1.67 us

profile of v3, /device:TPU:0, one launch (start us, length us, event | category | flops | bytes accessed | tf_op | source)
XLA Modules:
  0.0 49.5 jit_solution(5555162463847758923)
XLA Ops:
  0.6 0.0 copy-start
  0.6 1.0 %copy-done = f32[512,256]{1,0:T(8,128)S(1)} copy-done((f32[512,256]{1,0:T(8,128)S(1)}, f32[512,256]{1,0:T(8,128)}, u32[]{:S(2)}) %copy-start) | copy-done | bytes 524312
  1.7 0.0 copy-start.1
  1.7 0.9 %copy-done.1 = s32[65536]{0:T(1024)S(1)} copy-done((s32[65536]{0:T(1024)S(1)}, s32[65536]{0:T(1024)}, u32[]{:S(2)}) %copy-start.1) | copy-done | bytes 262168
  2.6 0.0 copy-start.2
  2.6 0.7 %copy-done.2 = s32[512]{0:T(512)S(1)} copy-done((s32[512]{0:T(512)S(1)}, s32[512]{0:T(512)}, u32[]{:S(2)}) %copy-start.2) | copy-done | bytes 2072
  3.3 0.0 copy-start.3
  3.3 0.7 %copy-done.3 = s32[512]{0:T(512)S(1)} copy-done((s32[512]{0:T(512)S(1)}, s32[512]{0:T(512)}, u32[]{:S(2)}) %copy-start.3) | copy-done | bytes 2072
  4.0 0.0 copy-start.4
  4.0 0.7 %copy-done.4 = s32[256]{0:T(256)S(1)} copy-done((s32[256]{0:T(256)S(1)}, s32[256]{0:T(256)}, u32[]{:S(2)}) %copy-start.4) | copy-done | bytes 1048
  4.7 41.9 %shard_map.84 = (f32[2048,256]{1,0:T(8,128)S(1)}, f32[8,2048]{1,0:T(8,128)S(1)}, f32[128,256]{1,0:T(8,128)S(1)}, f32[8,128]{1,0:T(8,128)S(1)}) custom-call(s32[1,512]{1,0:T(1,128)S(1)} %bitcast.9, s32[1,512]{1,0:T(1,128)S(1)} %bitcast.10, s32[1,256]{1,0:T(1,128)S(1)} %bitcast.11, s32[512,128]{1,0:T(8,128)S(1)} %bitcast.8, f32[512,256]{1,0:T(8,128)S(1)} %copy-done), custom_call_target="tpu_custom_call" | custom-call | tf_op jit(solution)/shard_map/pallas_call | solution.py:441
  46.5 0.5 %add_sqrt_fusion.1 = (f32[128]{0:T(128)S(1)}, f32[128]{0:T(128)}) fusion(f32[8,128]{1,0:T(8,128)S(1)} %get-tuple-element.11), kind=kLoop, calls=%fused_computation.3 | loop fusion | flops 128 | bytes 1536 | tf_op jit(solution)/shard_map/sqrt | solution.py:500
  47.1 0.7 %broadcast_divide_fusion.1 = f32[128,256]{1,0:T(8,128)} fusion(f32[128,256]{1,0:T(8,128)S(1)} %get-tuple-element.10, f32[128]{0:T(128)S(1)} %get-tuple-element.12), kind=kLoop, calls=%fused_computation.1 | loop fusion | flops 32768 | bytes 262656 | tf_op jit(solution)/shard_map/div | solution.py:500
  47.8 0.0 copy-start.5
  47.8 1.7 %broadcast_divide_fusion = f32[2048,256]{1,0:T(8,128)} fusion(f32[2048,256]{1,0:T(8,128)S(1)} %get-tuple-element.8, f32[2048]{0:T(1024)S(1)} %add_sqrt_fusion), kind=kLoop, calls=%fused_computation | loop fusion | flops 524288 | bytes 4202496 | tf_op jit(solution)/shard_map/div | solution.py:499
  49.5 0.0 copy-done.5
  (2 shorter events, 0.0 us)
Async XLA Ops:
  0.6 1.0 %copy-start = (f32[512,256]{1,0:T(8,128)S(1)}, f32[512,256]{1,0:T(8,128)}, u32[]{:S(2)}) copy-start(f32[512,256]{1,0:T(8,128)} %feat_hbm.1) | copy-start | bytes 1572868
  1.7 0.9 %copy-start.1 = (s32[65536]{0:T(1024)S(1)}, s32[65536]{0:T(1024)}, u32[]{:S(2)}) copy-start(s32[65536]{0:T(1024)} %param.8) | copy-start | bytes 786436
  2.6 0.7 %copy-start.2 = (s32[512]{0:T(512)S(1)}, s32[512]{0:T(512)}, u32[]{:S(2)}) copy-start(s32[512]{0:T(512)} %param.6) | copy-start | bytes 6148
  3.3 0.7 %copy-start.3 = (s32[512]{0:T(512)S(1)}, s32[512]{0:T(512)}, u32[]{:S(2)}) copy-start(s32[512]{0:T(512)} %param.7) | copy-start | bytes 6148
  4.0 0.7 %copy-start.4 = (s32[256]{0:T(256)S(1)}, s32[256]{0:T(256)}, u32[]{:S(2)}) copy-start(s32[256]{0:T(256)} %param.9) | copy-start | bytes 3076
  47.8 1.7 %copy-start.5 = (f32[1,2048]{1,0:T(1,128)}, f32[1,2048]{1,0:T(1,128)S(1)}, u32[]{:S(2)}) copy-start(f32[1,2048]{1,0:T(1,128)S(1)} %slice.6) | copy-start | bytes 24580
